TPU v7x, 256 devices: a whole 4x4x8 slice. The times are simulated.
256 devices in a mesh: rep: 16 (over z_hi, x), tp: 16 (over z_lo, y, core).
Axes of the slice: x: 4, y: 4, z: 8 (z_hi: 4, z_lo: 2; z = z_hi * 2 + z_lo), core: 2. Of those that a mesh axis runs over, the one named last changes fastest.
Arguments:
- tokens: bfloat16 [512, 4096], P(('rep', 'tp')), may hold values from -6 to 6
- conv_state: bfloat16 [3, 512, 8192], P(None, 'rep', 'tp'), may hold values from -6 to 6
- ssm_state: float32 [512, 16, 8192], P('rep', None, 'tp'), may hold values from -6 to 6
- norm_gains: bfloat16 [2, 4096], P(None, ('rep', 'tp')), may hold values from 0.5 to 1.5
- conv_weight: bfloat16 [4, 8192], P(None, ('rep', 'tp')), may hold values from -3 to 3
- conv_skip: bfloat16 [2, 8192], P(None, ('rep', 'tp')), may hold values from -3 to 3
- step_bias: bfloat16 [8192], P(('rep', 'tp')), may hold values from -5 to -1
- decay_log: bfloat16 [16, 8192], P(None, ('rep', 'tp')), may hold values from 0 to 2.796875
- input_proj: bfloat16 [4096, 2, 8192], P(('rep', 'tp')), may hold values from -0.09375 to 0.09375
- select_proj: bfloat16 [8192, 288], P('tp', 'rep'), may hold values from -0.0625 to 0.0625
- step_proj: bfloat16 [256, 8192], P(('rep', 'tp')), may hold values from -0.375 to 0.375
- output_proj: bfloat16 [8192, 4096], P(None, ('rep', 'tp')), may hold values from -0.0625 to 0.0625
- router: bfloat16 [4096, 16], P(('rep', 'tp')), may hold values from -0.09375 to 0.09375
- expert_proj: bfloat16 [4096, 2, 2, 12288], P(('rep', 'tp')), may hold values from -0.09375 to 0.09375
- expert_ids: int32 [512, 2], P(('rep', 'tp')), may hold values from 0 to 15, as said below
Outputs:
- mamba_out: bfloat16 [512, 4096], P(('rep', 'tp'))
- conv_next: bfloat16 [3, 512, 8192], P(None, 'rep', 'tp')
- ssm_next: float32 [512, 16, 8192], P('rep', None, 'tp')
- expert_hidden: bfloat16 [1024, 12288], P('rep', 'tp')
Inputs may be any that keep to these rules, and one draw needn't show every extreme that they name: `expert_ids`: each row names two different experts. Within each aligned block of 2 rows (the rows of one device) each expert e < 2 is named by at most 2 rows.
All inputs are finite; a program needn't handle non-finite values.
Results may differ from a plain program's by a relative error of at most 0.04.
Values may be sent and summed in bfloat16 or wider, within the bound.
A program may use at most 128 MiB of HBM per device.

v0:
```python
import math
import jax
import jax.numpy as jnp
from jax import lax
from jax.sharding import Mesh
from jax.sharding import PartitionSpec as P

CAPACITY = 2
REP_TP = ("rep_0", "rep_1", "tp")
REP = ("rep_0", "rep_1")
epsilon = 1e-05


def in_one_piece(arrays, axis, dim, along):
    widths = [a.shape[along] for a in arrays]
    both = jnp.concatenate(arrays, axis=along)
    out = lax.all_gather(both, axis, axis=dim, tiled=True)
    return tuple(jnp.split(out, [sum(widths[:k]) for k in range(1, len(widths))], axis=along))


def from_everyone(array, axis):
    devices = lax.axis_size(axis)
    return lax.all_to_all(
        jnp.broadcast_to(array[None], (devices, *array.shape)), axis, 0, 0, tiled=True
    )


def joined_along(blocks, dim):
    dims = list(blocks.shape[1:])
    dims[dim] *= blocks.shape[0]
    return jnp.moveaxis(blocks, 0, dim).reshape(dims)


def gathered_copies(array, axis, dim):
    blocks = from_everyone(array, axis)
    return joined_along(blocks, dim)


def gather_packed(arrays, axis, dims):
    ravelled = jnp.concatenate([a.reshape(-1) for a in arrays])
    lines, at, outs = (lax.all_gather(ravelled, axis), 0, [])
    for a, dim in zip(arrays, dims):
        blocks = lines[:, at : at + a.size].reshape(-1, *a.shape)
        outs.append(joined_along(blocks, dim))
        at += a.size
    return tuple(outs)


def over_copies(array, axis):
    return from_everyone(array, axis).astype(jnp.float32).sum(axis=0)


def split_up(array, dim, devices):
    before, after = (array.shape[:dim], array.shape[dim + 1 :])
    return jnp.moveaxis(array.reshape(*before, devices, -1, *after), dim, 0)


def sent_and_summed(array, axis, dim):
    devices = lax.axis_size(axis)
    blocks = lax.all_to_all(split_up(array, dim, devices), axis, 0, 0, tiled=True)
    return jnp.sum(blocks.astype(jnp.float32), axis=0)


def side_by_side(arrays, axis, dim, along):
    widths = [math.prod(a.shape[along:]) for a in arrays]
    both = jnp.concatenate(
        [a.reshape(*a.shape[:along], w) for a, w in zip(arrays, widths)], axis=along
    )
    out = lax.all_gather(both, axis, axis=dim, tiled=True)
    blocks = jnp.split(out, [sum(widths[:k]) for k in range(1, len(widths))], axis=along)
    return tuple((b.reshape(*out.shape[:along], *a.shape[along:]) for a, b in zip(arrays, blocks)))


def own_block(blocks, axes, order):
    dims = [lax.axis_size(a) for a in axes]
    blocks = blocks.reshape(*dims, *blocks.shape[1:])
    blocks = blocks.transpose(*order, *range(len(axes), blocks.ndim))
    blocks = blocks.reshape(-1, *blocks.shape[len(axes) :])
    for k in order:
        blocks = lax.psum_scatter(blocks, axes[k], scatter_dimension=0, tiled=True)
    return blocks[0]


def scatter_axes(array, axes, order, dim):
    devices = lax.axis_size(axes)
    return own_block(split_up(array, dim, devices), axes, order)


def norm_scale(values, gain):
    mean_square = jnp.mean(values * values, axis=-1, keepdims=True)
    return values * lax.rsqrt(mean_square + epsilon) * gain.astype(jnp.float32)


def shards(
    tokens,
    conv_state,
    ssm_state,
    norm_gains,
    conv_weight,
    conv_skip,
    step_bias,
    decay_log,
    input_proj,
    select_proj,
    step_proj,
    output_proj,
    router,
    expert_proj,
    expert_ids,
):
    tp_count = lax.axis_size("tp")
    tp_index = lax.axis_index("tp")
    norm_gain, conv_taps, skip_rows, shift_full, decay_full, router_full = (
        lax.all_gather(norm_gains, REP_TP, axis=1, tiled=True),
        *in_one_piece((conv_weight, conv_skip), REP_TP, 1, 0),
        lax.all_gather(step_bias, REP_TP, axis=0, tiled=True),
        lax.all_gather(decay_log, REP_TP, axis=1, tiled=True),
        lax.all_gather(router, REP_TP, axis=0, tiled=True),
    )
    inner_dev = ssm_state.shape[2]
    channel_start = tp_index * inner_dev
    conv_taps = lax.dynamic_slice_in_dim(conv_taps, channel_start, inner_dev, 1).astype(jnp.float32)
    skip_rows = lax.dynamic_slice_in_dim(skip_rows, channel_start, inner_dev, 1).astype(jnp.float32)
    shift_dev = lax.dynamic_slice_in_dim(shift_full, channel_start, inner_dev, 0).astype(
        jnp.float32
    )
    decay_dev = lax.dynamic_slice_in_dim(decay_full, channel_start, inner_dev, 1).astype(
        jnp.float32
    )
    model_rows = input_proj.shape[0]
    inner_all = input_proj.shape[2]
    input_blocks, expert_blocks, step_blocks = (
        lax.all_to_all(
            input_proj.reshape(model_rows, 1, 2, inner_all),
            "tp",
            split_axis=3,
            concat_axis=0,
            tiled=True,
        ),
        lax.all_to_all(expert_proj, "tp", split_axis=3, concat_axis=0, tiled=True),
        lax.all_to_all(
            step_proj.reshape(step_proj.shape[0], 1, 1, inner_all),
            "tp",
            split_axis=3,
            concat_axis=0,
            tiled=True,
        ),
    )
    output_blocks = lax.all_to_all(output_proj, "tp", split_axis=0, concat_axis=1, tiled=True)
    residual_in = tokens.astype(jnp.float32)
    normed = norm_scale(residual_in, norm_gain[0]).astype(jnp.bfloat16)
    features = gathered_copies(normed, "tp", 0)
    shard_piece = lax.all_gather(input_blocks, REP, axis=0, tiled=True)
    piece_rows = shard_piece.shape[0]
    projected = jnp.dot(
        features, shard_piece.reshape(piece_rows, 2 * inner_dev), preferred_element_type=jnp.float32
    )
    output_rows, step_rows, select_rows = gather_packed(
        (output_blocks, step_blocks, select_proj), REP, (1, 0, 1)
    )
    step_rows = step_rows.reshape(step_rows.shape[0], inner_dev)
    step_rank = step_rows.shape[0]
    state_count = ssm_state.shape[1]
    conv_input = projected[:, :inner_dev]
    gate_z = projected[:, inner_dev:]
    history = conv_state.astype(jnp.float32)
    conv_mix = (
        jnp.sum(conv_taps[:-1, None, :] * history, axis=0)
        + conv_taps[-1] * conv_input
        + skip_rows[0]
    )
    conv_next = jnp.concatenate([conv_state[1:], conv_input.astype(jnp.bfloat16)[None]], axis=0)
    activated = jax.nn.silu(conv_mix)
    select_part = jnp.dot(
        activated.astype(jnp.bfloat16), select_rows, preferred_element_type=jnp.float32
    )
    selected = over_copies(select_part.astype(jnp.bfloat16), "tp").astype(jnp.float32)
    step_low = selected[:, :step_rank].astype(jnp.bfloat16)
    input_map = selected[:, step_rank : step_rank + state_count]
    output_map = selected[:, step_rank + state_count :]
    step_size = jax.nn.softplus(
        jnp.dot(step_low, step_rows, preferred_element_type=jnp.float32) + shift_dev
    )
    decay_rate = -jnp.exp(decay_dev)
    factor = jnp.exp(step_size[:, None, :] * decay_rate[None])
    ssm_next = factor * ssm_state + (step_size * activated)[:, None, :] * input_map[:, :, None]
    readout = jnp.sum(ssm_next * output_map[:, :, None], axis=1) + skip_rows[1] * activated
    gated_out = (readout * jax.nn.silu(gate_z)).astype(jnp.bfloat16)
    output_part = jnp.dot(gated_out, output_rows, preferred_element_type=jnp.float32)
    mixer_out = sent_and_summed(output_part.astype(jnp.bfloat16), "tp", 0)
    residual = residual_in + mixer_out
    mamba_out = residual.astype(jnp.bfloat16)
    moe_in = norm_scale(residual, norm_gain[1]).astype(jnp.bfloat16)
    logits = jnp.dot(moe_in, router_full, preferred_element_type=jnp.float32)
    expert_total = logits.shape[1]
    choose = (
        expert_ids[:, :, None] == jnp.arange(expert_total, dtype=jnp.int32)[None, None, :]
    ).astype(jnp.float32)
    picked = jnp.sum(choose * logits[:, None, :], axis=2)
    first_gate = jax.nn.sigmoid(picked[:, 0] - picked[:, 1])
    second_gate = jax.nn.sigmoid(picked[:, 1] - picked[:, 0])
    window_count = expert_blocks.shape[1]
    window = jnp.arange(window_count, dtype=jnp.int32)
    names_first = expert_ids[:, 0:1] == window[None, :]
    names_second = expert_ids[:, 1:2] == window[None, :]
    zero = jnp.zeros((), jnp.float32)
    gate_w = jnp.where(names_first, first_gate[:, None], zero) + jnp.where(
        names_second, second_gate[:, None], zero
    )
    routed = (names_first | names_second).astype(jnp.int32)
    position = jnp.cumsum(routed, axis=0) - routed
    slot_of = (position[:, :, None] == jnp.arange(CAPACITY, dtype=jnp.int32)[None, None, :]) & (
        routed[:, :, None] > 0
    )
    slot_x = jnp.einsum(
        "tec,td->ecd", slot_of.astype(jnp.bfloat16), moe_in, preferred_element_type=jnp.float32
    )
    slot_local = window_count * CAPACITY
    slot_x = slot_x.astype(jnp.bfloat16).reshape(slot_local, moe_in.shape[1])
    slot_gate = (
        jnp.einsum("tec,te->ec", slot_of.astype(jnp.float32), gate_w)
        .astype(jnp.bfloat16)
        .reshape(slot_local)
    )
    feature_rows = expert_blocks.shape[0]
    replica_rows, gate_all = side_by_side((slot_x, slot_gate), "tp", 0, 1)
    gathered = lax.all_to_all(replica_rows, REP, split_axis=1, concat_axis=0, tiled=True)
    hidden_dev = expert_blocks.shape[3]
    group_rows = tp_count * slot_local
    picked_rows = gathered
    picked_rows = picked_rows.reshape(
        group_rows * lax.axis_size(REP) // slot_local, window_count, CAPACITY, feature_rows
    )
    product = jnp.einsum(
        "gecd,dexf->gecxf", picked_rows, expert_blocks, preferred_element_type=jnp.float32
    )
    summed = scatter_axes(
        product.reshape(group_rows * lax.axis_size(REP), 2 * hidden_dev).astype(jnp.bfloat16),
        REP,
        (1, 0),
        0,
    ).astype(jnp.float32)
    hidden = (
        gate_all.astype(jnp.float32)[:, None]
        * jax.nn.silu(summed[:, :hidden_dev])
        * summed[:, hidden_dev:]
    )
    expert_hidden = hidden.astype(jnp.bfloat16)
    return (mamba_out, conv_next, ssm_next, expert_hidden)


def solution(mesh):
    split = Mesh(mesh.devices.reshape(4, 4, mesh.shape["tp"]), ("rep_0", "rep_1", "tp"))
    return jax.shard_map(
        shards,
        mesh=split,
        in_specs=(
            P(REP_TP, None),
            P(None, REP, "tp"),
            P(REP, None, "tp"),
            P(None, REP_TP),
            P(None, REP_TP),
            P(None, REP_TP),
            P(REP_TP),
            P(None, REP_TP),
            P(REP_TP, None, None),
            P("tp", REP),
            P(REP_TP, None),
            P(None, REP_TP),
            P(REP_TP, None),
            P(REP_TP, None, None, None),
            P(REP_TP, None),
        ),
        out_specs=(P(REP_TP, None), P(None, REP, "tp"), P(REP, None, "tp"), P(REP, "tp")),
        check_vma=False,
    )
```

profile of v0, /device:TPU:2, one launch (start us, length us, event | category | flops | bytes accessed | tf_op | source)
XLA Modules:
  0.0 1973.0 jit_solution(4106802272947335639)
XLA Ops:
  7.2 8.3 copy.135
  16.0 62.6 %reduce.12 = bf16[8192]{0:T(1024)(128)(2,1)S(1)} reduce(bf16[8192,1,1,1]{3,2,1,0:T(2,128)(2,1)} %bitcast.104, bf16[]{:T(256)} %broadcast.160), dimensions={1,2,3}, to_apply=%bitcast.77.reduce_sub_computation | reduce | bytes 32770
  95.0 8.4 reshape.274
  103.4 62.0 %bitcast_reduce_fusion = bf16[8192]{0:T(1024)(128)(2,1)S(1)} fusion(bf16[8192,1,1,1]{3,2,1,0:T(2,128)(2,1)} %reshape.274), kind=kLoop, calls=%fused_computation.72 | loop fusion | bytes 32768 | tf_op jit(solution)/shard_map/all_to_all | solution.py:141
  169.6 6.8 copy.129
  176.3 7.7 bitcast_bitcast_fusion
  189.8 18.9 all_to_all.92
  212.8 10.3 copy.152
  223.2 333.4 %all-gather.2 = bf16[256,16,2]{1,2,0:T(2,128)(2,1)S(1)} all-gather(bf16[1,16,2]{1,2,0:T(2,128)(2,1)S(1)} %bitcast.128), channel_id=1, replica_groups=mesh['rep_0'=4,'rep_1'=4,'tp'=16] {'rep_0','rep_1','tp'}, dimensions={0}, use_global_device_ids=true | all-gather | bytes 16448 | tf_op jit(solution)/shard_map/all_gather | solution.py:114
  561.5 342.0 %all-gather.1 = bf16[256,32,6]{1,2,0:T(8,128)(2,1)S(1)} all-gather(bf16[1,32,6]{1,2,0:T(8,128)(2,1)S(1)} %maximum_bitcast_fusion.1), channel_id=1, replica_groups=mesh['rep_0'=4,'rep_1'=4,'tp'=16] {'rep_0','rep_1','tp'}, dimensions={0}, use_global_device_ids=true | all-gather | bytes 98688 | tf_op jit(solution)/shard_map/all_gather | solution.py:17
  916.6 11.3 copy.132
  927.9 6.0 fusion.24
  938.5 344.1 %all-gather.3 = bf16[256,32,16]{1,2,0:T(8,128)(2,1)S(1)} all-gather(bf16[1,32,16]{1,2,0:T(8,128)(2,1)S(1)} %bitcast.126), channel_id=1, replica_groups=mesh['rep_0'=4,'rep_1'=4,'tp'=16] {'rep_0','rep_1','tp'}, dimensions={0}, use_global_device_ids=true | all-gather | bytes 263168 | tf_op jit(solution)/shard_map/all_gather | solution.py:117
  1284.3 98.4 %all-reduce = bf16[8192]{0:T(1024)(128)(2,1)S(1)} all-reduce(bf16[8192]{0:T(1024)(128)(2,1)S(1)} %dynamic-update-slice), channel_id=1, replica_groups=mesh['rep_0'=4,'rep_1'=4,'tp'=16] {'rep_0','rep_1','tp'}, use_global_device_ids=true, to_apply=%add | all-reduce | flops 8192 | bytes 32768
  1392.6 6.5 copy.139
  1410.8 20.2 %copy.142 = bf16[16,2,2,12288]{0,2,1,3:T(2,128)(2,1)} copy(bf16[16,2,2,12288]{3,2,1,0:T(2,128)(2,1)S(1)} %copy-done.1) | data formatting | bytes 3145728 | tf_op args[13]
  1430.9 17.7 reshape.277
  1448.6 328.0 %all_gather.34 = bf16[4096,16]{1,0:T(8,128)(2,1)S(1)} all-gather(bf16[16,16]{1,0:T(8,128)(2,1)S(1)} %copy-done.10), channel_id=1, replica_groups=mesh['rep_0'=4,'rep_1'=4,'tp'=16] {'rep_0','rep_1','tp'}, dimensions={0}, use_global_device_ids=true | all-gather | bytes 131584 | tf_op jit(solution)/shard_map/all_gather | solution.py:118
  1782.5 32.2 %all-gather.4 = bf16[16,4,4097]{2,1,0:T(4,128)(2,1)S(1)} all-gather(bf16[1,4,4097]{2,1,0:T(4,128)(2,1)S(1)} %maximum_bitcast_fusion), channel_id=1, replica_groups=mesh['rep_0'=4,'rep_1'=4,'tp'=16] {'tp'}, dimensions={0}, use_global_device_ids=true | all-gather | bytes 557192 | tf_op jit(solution)/shard_map/all_gather | solution.py:69
  1816.0 25.0 %all-to-all-start.6 = ((bf16[64,16,256]{2,0,1:T(8,128)(2,1)}), bf16[64,16,256]{2,0,1:T(8,128)(2,1)S(1)}, u32[]{:S(2)}, u32[]{:S(2)}) async-start(bf16[64,16,256]{2,0,1:T(8,128)(2,1)} %bitcast.95), calls=%async_computation.6 | async-start | bytes 1048576 | tf_op jit(solution)/shard_map/all_to_all | solution.py:227
  1841.1 12.1 reshape.278
  1853.2 26.5 %copy.143 = bf16[16,2,2,16,768]{4,0,3,2,1:T(8,128)(2,1)S(1)} copy(bf16[16,2,2,16,768]{0,2,1,4,3:T(2,128)(2,1)} %bitcast.98) | data formatting | bytes 3145728 | tf_op jit(solution)/shard_map/all_to_all | solution.py:140
  1891.5 39.0 %reduce-scatter.3.cloned.1.call-done = bf16[4,64,1536]{2,1,0:T(8,128)(2,1)} async-done(((bf16[16,64,1536]{2,1,0:T(8,128)(2,1)}), bf16[4,64,1536]{2,1,0:T(8,128)(2,1)}) %reduce-scatter.3.cloned.1.call-update) | async-done | bytes 786448 | tf_op jit(solution)/shard_map/reduce_scatter | solution.py:80
  1932.0 32.7 %reduce-scatter.5.cloned.1.call-done = bf16[1,64,1536]{2,1,0:T(8,128)(2,1)} async-done(((bf16[4,64,1536]{2,1,0:T(8,128)(2,1)}), bf16[1,64,1536]{2,1,0:T(8,128)(2,1)}) %reduce-scatter.5.cloned.1.call-update) | async-done | bytes 196624 | tf_op jit(solution)/shard_map/reduce_scatter | solution.py:80
  (139 shorter events, 98.6 us)
Async XLA Ops:
  7.2 78.0 %copy-start.6 = (bf16[8192,16]{0,1:T(8,128)(2,1)S(1)}, bf16[8192,16]{0,1:T(8,128)(2,1)}, u32[]{:S(2)}) copy-start(bf16[8192,16]{0,1:T(8,128)(2,1)} %param.26) | copy-start | bytes 786436
  7.2 78.7 %copy-start.7 = (bf16[512,18]{0,1:T(8,128)(2,1)S(1)}, bf16[512,18]{0,1:T(8,128)(2,1)}, u32[]{:S(2)}) copy-start(bf16[512,18]{0,1:T(8,128)(2,1)} %param.24) | copy-start | bytes 55300
  79.2 12.0 all-to-all-start.3
  91.2 74.2 %all-to-all-start.2 = ((bf16[16,512,16]{1,2,0:T(8,128)(2,1)}), bf16[16,512,16]{1,2,0:T(8,128)(2,1)S(1)}, u32[]{:S(2)}, u32[]{:S(2)}) async-start(bf16[16,512,16]{1,2,0:T(8,128)(2,1)} %bitcast.96), calls=%async_computation.2 | async-start | bytes 524288 | tf_op jit(solution)/shard_map/all_to_all | solution.py:149
  94.8 809.6 %all-gather.10.cloned.1.call-start = ((), (), s32[]{:S(2)}) async-start(), calls=%async_computation.13 | async-start | bytes 5048320 | tf_op jit(solution)/shard_map/all_gather | solution.py:41
  103.4 66.2 %copy-start.3 = (bf16[16,2,8192]{2,1,0:T(2,128)(2,1)S(1)}, bf16[16,2,8192]{2,1,0:T(2,128)(2,1)}, u32[]{:S(2)}) copy-start(bf16[16,2,8192]{2,1,0:T(2,128)(2,1)} %param.23) | copy-start | bytes 1572868
  169.5 747.1 %all-gather.8.cloned.1.call-start = ((), (), s32[]{:S(2)}) async-start(), calls=%async_computation.10 | async-start | bytes 8912896 | tf_op jit(solution)/shard_map/all_gather | solution.py:153
  208.7 14.5 copy-start.12
  208.7 348.1 %copy-start.5 = (bf16[2,4096]{1,0:T(2,128)(2,1)S(1)}, bf16[2,4096]{1,0:T(2,128)(2,1)}, u32[]{:S(2)}) copy-start(bf16[2,4096]{1,0:T(2,128)(2,1)} %param.15) | copy-start | bytes 49156
  212.8 348.7 %copy-start.11 = (bf16[4,32]{1,0:T(4,128)(2,1)S(1)}, bf16[4,32]{1,0:T(4,128)(2,1)}, u32[]{:S(2)}) copy-start(bf16[4,32]{1,0:T(4,128)(2,1)} %param.19) | copy-start | bytes 772
  212.8 348.7 %copy-start.13 = (bf16[2,32]{1,0:T(2,128)(2,1)S(1)}, bf16[2,32]{1,0:T(2,128)(2,1)}, u32[]{:S(2)}) copy-start(bf16[2,32]{1,0:T(2,128)(2,1)} %param.20) | copy-start | bytes 388
  212.8 691.3 %copy-start.4 = (bf16[3,32,512]{2,1,0:T(8,128)(2,1)S(1)}, bf16[3,32,512]{2,1,0:T(8,128)(2,1)}, u32[]{:S(2)}) copy-start(bf16[3,32,512]{2,1,0:T(8,128)(2,1)} %param.16) | copy-start | bytes 294916
  558.0 346.2 %all-to-all-start = ((bf16[16,2,4096]{2,1,0:T(2,128)(2,1)}), bf16[16,2,4096]{2,1,0:T(2,128)(2,1)S(1)}, u32[]{:S(2)}, u32[]{:S(2)}) async-start(bf16[16,2,4096]{2,1,0:T(2,128)(2,1)} %broadcast_in_dim.24), calls=%async_computation | async-start | bytes 524288 | tf_op jit(solution)/shard_map/all_to_all | solution.py:23
  933.9 350.1 %copy-start.14 = (bf16[32]{0:T(256)(128)(2,1)S(1)}, bf16[32]{0:T(256)(128)(2,1)}, u32[]{:S(2)}) copy-start(bf16[32]{0:T(256)(128)(2,1)} %param.21) | copy-start | bytes 196
  933.9 448.8 %copy-start.8 = (s32[2,2]{1,0:T(2,128)S(1)}, s32[2,2]{1,0:T(2,128)}, u32[]{:S(2)}) copy-start(s32[2,2]{1,0:T(2,128)} %param.29) | copy-start | bytes 52
  934.9 464.2 %all-to-all-start.4 = ((bf16[16,32,288]{2,1,0:T(8,128)(2,1)}), bf16[16,32,288]{2,1,0:T(8,128)(2,1)S(1)}, u32[]{:S(2)}, u32[]{:S(2)}) async-start(bf16[16,32,288]{2,1,0:T(8,128)(2,1)} %broadcast_in_dim.25), calls=%async_computation.4 | async-start | bytes 786432 | tf_op jit(solution)/shard_map/all_to_all | solution.py:23
  1405.3 371.3 %all-to-all-start.5 = ((bf16[16,2,4096]{2,1,0:T(2,128)(2,1)}), bf16[16,2,4096]{2,1,0:T(2,128)(2,1)S(1)}, u32[]{:S(2)}, u32[]{:S(2)}) async-start(bf16[16,2,4096]{2,1,0:T(2,128)(2,1)} %reshape.243), calls=%async_computation.5 | async-start | bytes 524288 | tf_op jit(solution)/shard_map/all_to_all | solution.py:60
  1430.9 17.7 copy-start.10
  1776.6 39.4 %all-to-all-start.7 = ((bf16[16,2,24576]{2,1,0:T(2,128)(2,1)}), bf16[16,2,24576]{2,1,0:T(2,128)(2,1)S(1)}, u32[]{:S(2)}, u32[]{:S(2)}) async-start(bf16[16,2,24576]{2,1,0:T(2,128)(2,1)} %reshape.277), calls=%async_computation.7 | async-start | bytes 3145728 | tf_op jit(solution)/shard_map/all_to_all | solution.py:140
  1815.0 38.2 %copy-start = (bf16[64,4097]{1,0:T(8,128)(2,1)}, bf16[64,4097]{1,0:T(8,128)(2,1)S(1)}, u32[]{:S(2)}) copy-start(bf16[64,4097]{1,0:T(8,128)(2,1)S(1)} %reshape.261) | copy-start | bytes 1573252
  1816.0 63.7 %all-to-all-start.6 = ((bf16[64,16,256]{2,0,1:T(8,128)(2,1)}), bf16[64,16,256]{2,0,1:T(8,128)(2,1)S(1)}, u32[]{:S(2)}, u32[]{:S(2)}) async-start(bf16[64,16,256]{2,0,1:T(8,128)(2,1)} %bitcast.95), calls=%async_computation.6 | async-start | bytes 1048576 | tf_op jit(solution)/shard_map/all_to_all | solution.py:227
  1841.0 89.4 %reduce-scatter.3.cloned.1.call-start = ((), (), s32[]{:S(2)}) async-start(), calls=%async_computation.11 | async-start | bytes 3932160 | tf_op jit(solution)/shard_map/reduce_scatter | solution.py:80
  1887.5 43.0 %slice-start.1 = ((bf16[3,32,512]{2,1,0:T(8,128)(2,1)}), bf16[2,32,512]{2,1,0:T(8,128)(2,1)S(1)}, s32[]{:S(2)}) async-start(bf16[3,32,512]{2,1,0:T(8,128)(2,1)} %param.16), calls=%async_computation.15 | async-start | bytes 131072 | tf_op jit(solution)/shard_map/slice | solution.py:172
  1891.4 73.2 %reduce-scatter.5.cloned.1.call-start = ((), (), s32[]{:S(2)}) async-start(), calls=%async_computation.12 | async-start | bytes 983040 | tf_op jit(solution)/shard_map/reduce_scatter | solution.py:80
  (4 other events, 33.4 us)
Sparse Core Ops, SparseCore 0:
  169.6 81.2 all-gather.9
  253.9 117.8 all-gather.7
  1891.5 38.8 reduce-scatter.2
  1932.9 31.7 reduce-scatter.4
where the time goes:
time: 1980 us; the launch traced here: 1970 us
  blocking collectives  1500 us (76%)
  local copies, waits for them, and re-layouts  252 us (13%)
  waiting for transfers between devices  76.8 us (4%)
  other arithmetic  70.1 us (4%)
  starting transfers between devices  51.1 us (3%)
    all_gather x1, blocking collectives, shards(): lax.all_gather(decay_log, REP_TP, axis=1, tiled=True)  344 us
    all_gather x1, blocking collectives, in_one_piece(): out = lax.all_gather(both, axis, axis=dim, tiled=True)  342 us
    all_gather x1, blocking collectives, shards(): lax.all_gather(norm_gains, REP_TP, axis=1, tiled=True)  333 us
    all_gather x1, blocking collectives, shards(): lax.all_gather(router, REP_TP, axis=0, tiled=True)  328 us
    unnamed x1, blocking collectives  98.4 us
    unnamed x48, local copies, waits for them, and re-layouts  91.4 us
    reduce_scatter x2, waiting for transfers between devices, own_block(): blocks = lax.psum_scatter(blocks, axes[k], scatter_dimension=0, tiled=True)  71.6 us
    unnamed x3, other arithmetic  62.6 us
  transfers between devices with their start and end apart: 11, of which 3 were waited for; matrix products, arithmetic and copies ran while one was open for 11% of the time, Pallas kernels for 0%

commit v1 on v0

--- a/solution.py
+++ b/solution.py
@@ -114,7 +114,9 @@
         lax.all_gather(norm_gains, REP_TP, axis=1, tiled=True),
         *in_one_piece((conv_weight, conv_skip), REP_TP, 1, 0),
         lax.all_gather(step_bias, REP_TP, axis=0, tiled=True),
-        lax.all_gather(decay_log, REP_TP, axis=1, tiled=True),
+        jnp.concatenate(
+            lax.all_to_all(jnp.stack([decay_log] * lax.axis_size(REP_TP)), REP_TP, 0, 0), axis=1
+        ),
         lax.all_gather(router, REP_TP, axis=0, tiled=True),
     )
     inner_dev = ssm_state.shape[2]

time: 1980 us -> 1650 us (0.83)
  blocking collectives: 1500 us -> 1130 us
  starting transfers between devices: 51.1 us -> 79.7 us
    all_gather x1 -> x0, blocking collectives: 344 us -> none  [shards(): lax.all_gather(decay_log, REP_TP, axis=1, tiled=True)]
    all_to_all x0 -> x1, starting transfers between devices: none -> 27.8 us  [shards(): lax.all_to_all(jnp.stack([decay_log] * lax.axis_size(REP_TP)), REP_TP, 0, 0)]
    unnamed x1, blocking collectives: 98.4 us -> 77.6 us
    unnamed x48 -> x47, local copies, waits for them, and re-layouts: 91.4 us -> 92.1 us
  transfers between devices with their start and end apart: 11 -> 12, of which waited for: 3 -> 3; matrix products, arithmetic and copies ran while one was open for 11% -> 15% of each run, Pallas kernels for 0% -> 0%
where the time goes in v1:
time: 1650 us; the launch traced here: 1640 us
  blocking collectives  1130 us (68%)
  local copies, waits for them, and re-layouts  255 us (15%)
  starting transfers between devices  79.7 us (5%)
  waiting for transfers between devices  76.7 us (5%)
  other arithmetic  71.4 us (4%)
    all_gather x1, blocking collectives, in_one_piece(): out = lax.all_gather(both, axis, axis=dim, tiled=True)  342 us
    all_gather x1, blocking collectives, shards(): lax.all_gather(norm_gains, REP_TP, axis=1, tiled=True)  334 us
    all_gather x1, blocking collectives, shards(): lax.all_gather(router, REP_TP, axis=0, tiled=True)  327 us
    unnamed x47, local copies, waits for them, and re-layouts  92.1 us
    unnamed x1, blocking collectives  77.6 us
    reduce_scatter x2, waiting for transfers between devices, own_block(): blocks = lax.psum_scatter(blocks, axes[k], scatter_dimension=0, tiled=True)  71.6 us
    unnamed x3, other arithmetic  62.6 us
    all_to_all x1, local copies, waits for them, and re-layouts, shards(): lax.all_to_all(step_proj.reshape(step_proj.shape[0], 1, 1, inner_all), 't...  62 us
  transfers between devices with their start and end apart: 12, of which 3 were waited for; matrix products, arithmetic and copies ran while one was open for 15% of the time, Pallas kernels for 0%

profile of v1, /device:TPU:2, one launch (start us, length us, event | category | flops | bytes accessed | tf_op | source)
XLA Modules:
  0.0 1640.1 jit_solution(10133290462967937709)
XLA Ops:
  7.2 8.3 copy.133
  16.0 62.6 %reduce.12 = bf16[8192]{0:T(1024)(128)(2,1)S(1)} reduce(bf16[8192,1,1,1]{3,2,1,0:T(2,128)(2,1)} %bitcast.98, bf16[]{:T(256)} %broadcast.162), dimensions={1,2,3}, to_apply=%bitcast.71.reduce_sub_computation | reduce | bytes 32770
  95.0 8.4 reshape.282
  103.4 62.0 %bitcast_reduce_fusion = bf16[8192]{0:T(1024)(128)(2,1)S(1)} fusion(bf16[8192,1,1,1]{3,2,1,0:T(2,128)(2,1)} %reshape.282), kind=kLoop, calls=%fused_computation.72 | loop fusion | bytes 32768 | tf_op jit(solution)/shard_map/all_to_all | solution.py:143
  169.6 6.7 copy.127
  176.3 7.7 bitcast_bitcast_fusion
  189.8 18.9 %all_to_all.97 = bf16[16,2,8192]{2,1,0:T(2,128)(2,1)S(1)} all-to-all(bf16[16,2,8192]{2,1,0:T(2,128)(2,1)S(1)} %reshape.283), channel_id=1, replica_groups=mesh['rep_0'=4,'rep_1'=4,'tp'=16] {'tp'}, dimensions={0} | all-to-all | bytes 1048576 | tf_op jit(solution)/shard_map/all_to_all | solution.py:135
  212.8 10.3 copy.150
  223.2 333.8 %all-gather.2 = bf16[256,16,2]{1,2,0:T(2,128)(2,1)S(1)} all-gather(bf16[1,16,2]{1,2,0:T(2,128)(2,1)S(1)} %bitcast.122), channel_id=1, replica_groups=mesh['rep_0'=4,'rep_1'=4,'tp'=16] {'rep_0','rep_1','tp'}, dimensions={0}, use_global_device_ids=true | all-gather | bytes 16448 | tf_op jit(solution)/shard_map/all_gather | solution.py:114
  561.9 342.0 %all-gather.1 = bf16[256,32,6]{1,2,0:T(8,128)(2,1)S(1)} all-gather(bf16[1,32,6]{1,2,0:T(8,128)(2,1)S(1)} %maximum_bitcast_fusion.1), channel_id=1, replica_groups=mesh['rep_0'=4,'rep_1'=4,'tp'=16] {'rep_0','rep_1','tp'}, dimensions={0}, use_global_device_ids=true | all-gather | bytes 98688 | tf_op jit(solution)/shard_map/all_gather | solution.py:17
  906.1 27.8 %all-to-all-start.5 = ((bf16[256,2,256]{2,1,0:T(2,128)(2,1)}), bf16[256,2,256]{2,1,0:T(2,128)(2,1)S(1)}, u32[]{:S(2)}, u32[]{:S(2)}) async-start(bf16[256,2,256]{2,1,0:T(2,128)(2,1)} %reshape.285), calls=%async_computation.5 | async-start | bytes 524288 | tf_op jit(solution)/shard_map/all_to_all | solution.py:118
  946.3 12.0 copy.130
  958.3 6.0 fusion.24
  971.2 77.6 %all-reduce = bf16[8192]{0:T(1024)(128)(2,1)S(1)} all-reduce(bf16[8192]{0:T(1024)(128)(2,1)S(1)} %dynamic-update-slice), channel_id=1, replica_groups=mesh['rep_0'=4,'rep_1'=4,'tp'=16] {'rep_0','rep_1','tp'}, use_global_device_ids=true, to_apply=%add | all-reduce | flops 8192 | bytes 32768
  1060.6 6.4 copy.137
  1079.0 20.2 %copy.140 = bf16[16,2,2,12288]{0,2,1,3:T(2,128)(2,1)} copy(bf16[16,2,2,12288]{3,2,1,0:T(2,128)(2,1)S(1)} %copy-done.1) | data formatting | bytes 3145728 | tf_op args[13]
  1099.2 17.7 %reshape.287 = bf16[16,2,24576]{2,1,0:T(2,128)(2,1)} reshape(bf16[12288,2,2,16]{3,2,1,0:T(2,128)(2,1)} %bitcast.93) | data formatting | bytes 3145728
  1116.8 327.1 %all_gather.30 = bf16[4096,16]{1,0:T(8,128)(2,1)S(1)} all-gather(bf16[16,16]{1,0:T(8,128)(2,1)S(1)} %copy-done.9), channel_id=1, replica_groups=mesh['rep_0'=4,'rep_1'=4,'tp'=16] {'rep_0','rep_1','tp'}, dimensions={0}, use_global_device_ids=true | all-gather | bytes 131584 | tf_op jit(solution)/shard_map/all_gather | solution.py:120
  1449.7 32.2 %all-gather.3 = bf16[16,4,4097]{2,1,0:T(4,128)(2,1)S(1)} all-gather(bf16[1,4,4097]{2,1,0:T(4,128)(2,1)S(1)} %maximum_bitcast_fusion), channel_id=1, replica_groups=mesh['rep_0'=4,'rep_1'=4,'tp'=16] {'tp'}, dimensions={0}, use_global_device_ids=true | all-gather | bytes 557192 | tf_op jit(solution)/shard_map/all_gather | solution.py:69
  1483.2 25.0 %all-to-all-start.7 = ((bf16[64,16,256]{2,0,1:T(8,128)(2,1)}), bf16[64,16,256]{2,0,1:T(8,128)(2,1)S(1)}, u32[]{:S(2)}, u32[]{:S(2)}) async-start(bf16[64,16,256]{2,0,1:T(8,128)(2,1)} %bitcast.89), calls=%async_computation.7 | async-start | bytes 1048576 | tf_op jit(solution)/shard_map/all_to_all | solution.py:229
  1508.3 12.1 reshape.288
  1520.4 26.5 %copy.141 = bf16[16,2,2,16,768]{4,0,3,2,1:T(8,128)(2,1)S(1)} copy(bf16[16,2,2,16,768]{0,2,1,4,3:T(2,128)(2,1)} %bitcast.92) | data formatting | bytes 3145728 | tf_op jit(solution)/shard_map/all_to_all | solution.py:142
  1558.6 38.9 %reduce-scatter.3.cloned.1.call-done = bf16[4,64,1536]{2,1,0:T(8,128)(2,1)} async-done(((bf16[16,64,1536]{2,1,0:T(8,128)(2,1)}), bf16[4,64,1536]{2,1,0:T(8,128)(2,1)}) %reduce-scatter.3.cloned.1.call-update) | async-done | bytes 786448 | tf_op jit(solution)/shard_map/reduce_scatter | solution.py:80
  1599.1 32.6 %reduce-scatter.5.cloned.1.call-done = bf16[1,64,1536]{2,1,0:T(8,128)(2,1)} async-done(((bf16[4,64,1536]{2,1,0:T(8,128)(2,1)}), bf16[1,64,1536]{2,1,0:T(8,128)(2,1)}) %reduce-scatter.5.cloned.1.call-update) | async-done | bytes 196624 | tf_op jit(solution)/shard_map/reduce_scatter | solution.py:80
  (141 shorter events, 102.7 us)
Async XLA Ops:
  7.2 78.0 %copy-start.5 = (bf16[8192,16]{0,1:T(8,128)(2,1)S(1)}, bf16[8192,16]{0,1:T(8,128)(2,1)}, u32[]{:S(2)}) copy-start(bf16[8192,16]{0,1:T(8,128)(2,1)} %param.26) | copy-start | bytes 786436
  7.2 78.7 %copy-start.6 = (bf16[512,18]{0,1:T(8,128)(2,1)S(1)}, bf16[512,18]{0,1:T(8,128)(2,1)}, u32[]{:S(2)}) copy-start(bf16[512,18]{0,1:T(8,128)(2,1)} %param.24) | copy-start | bytes 55300
  79.2 12.0 all-to-all-start.3
  91.3 74.2 %all-to-all-start.2 = ((bf16[16,512,16]{1,2,0:T(8,128)(2,1)}), bf16[16,512,16]{1,2,0:T(8,128)(2,1)S(1)}, u32[]{:S(2)}, u32[]{:S(2)}) async-start(bf16[16,512,16]{1,2,0:T(8,128)(2,1)} %bitcast.90), calls=%async_computation.2 | async-start | bytes 524288 | tf_op jit(solution)/shard_map/all_to_all | solution.py:151
  94.8 839.3 %all-gather.9.cloned.1.call-start = ((), (), s32[]{:S(2)}) async-start(), calls=%async_computation.14 | async-start | bytes 5048320 | tf_op jit(solution)/shard_map/all_gather | solution.py:41
  103.4 66.2 %copy-start.2 = (bf16[16,2,8192]{2,1,0:T(2,128)(2,1)S(1)}, bf16[16,2,8192]{2,1,0:T(2,128)(2,1)}, u32[]{:S(2)}) copy-start(bf16[16,2,8192]{2,1,0:T(2,128)(2,1)} %param.23) | copy-start | bytes 1572868
  169.5 776.8 %all-gather.7.cloned.1.call-start = ((), (), s32[]{:S(2)}) async-start(), calls=%async_computation.11 | async-start | bytes 8912896 | tf_op jit(solution)/shard_map/all_gather | solution.py:155
  208.7 348.5 %copy-start.4 = (bf16[2,4096]{1,0:T(2,128)(2,1)S(1)}, bf16[2,4096]{1,0:T(2,128)(2,1)}, u32[]{:S(2)}) copy-start(bf16[2,4096]{1,0:T(2,128)(2,1)} %param.15) | copy-start | bytes 49156
  212.8 349.1 %copy-start.10 = (bf16[4,32]{1,0:T(4,128)(2,1)S(1)}, bf16[4,32]{1,0:T(4,128)(2,1)}, u32[]{:S(2)}) copy-start(bf16[4,32]{1,0:T(4,128)(2,1)} %param.19) | copy-start | bytes 772
  212.8 349.1 %copy-start.12 = (bf16[2,32]{1,0:T(2,128)(2,1)S(1)}, bf16[2,32]{1,0:T(2,128)(2,1)}, u32[]{:S(2)}) copy-start(bf16[2,32]{1,0:T(2,128)(2,1)} %param.20) | copy-start | bytes 388
  212.8 691.7 %copy-start.8 = (bf16[16,32]{1,0:T(8,128)(2,1)S(1)}, bf16[16,32]{1,0:T(8,128)(2,1)}, u32[]{:S(2)}) copy-start(bf16[16,32]{1,0:T(8,128)(2,1)} %param.22) | copy-start | bytes 3076
  223.1 683.0 %copy-start.3 = (bf16[3,32,512]{2,1,0:T(8,128)(2,1)S(1)}, bf16[3,32,512]{2,1,0:T(8,128)(2,1)}, u32[]{:S(2)}) copy-start(bf16[3,32,512]{2,1,0:T(8,128)(2,1)} %param.16) | copy-start | bytes 294916
  558.4 347.7 %all-to-all-start = ((bf16[16,2,4096]{2,1,0:T(2,128)(2,1)}), bf16[16,2,4096]{2,1,0:T(2,128)(2,1)S(1)}, u32[]{:S(2)}, u32[]{:S(2)}) async-start(bf16[16,2,4096]{2,1,0:T(2,128)(2,1)} %broadcast_in_dim.24), calls=%async_computation | async-start | bytes 524288 | tf_op jit(solution)/shard_map/all_to_all | solution.py:23
  906.1 58.5 %all-to-all-start.5 = ((bf16[256,2,256]{2,1,0:T(2,128)(2,1)}), bf16[256,2,256]{2,1,0:T(2,128)(2,1)S(1)}, u32[]{:S(2)}, u32[]{:S(2)}) async-start(bf16[256,2,256]{2,1,0:T(2,128)(2,1)} %reshape.285), calls=%async_computation.5 | async-start | bytes 524288 | tf_op jit(solution)/shard_map/all_to_all | solution.py:118
  958.3 90.5 %copy-start.7 = (s32[2,2]{1,0:T(2,128)S(1)}, s32[2,2]{1,0:T(2,128)}, u32[]{:S(2)}) copy-start(s32[2,2]{1,0:T(2,128)} %param.29) | copy-start | bytes 52
  965.4 101.7 %all-to-all-start.4 = ((bf16[16,32,288]{2,1,0:T(8,128)(2,1)}), bf16[16,32,288]{2,1,0:T(8,128)(2,1)S(1)}, u32[]{:S(2)}, u32[]{:S(2)}) async-start(bf16[16,32,288]{2,1,0:T(8,128)(2,1)} %broadcast_in_dim.25), calls=%async_computation.4 | async-start | bytes 786432 | tf_op jit(solution)/shard_map/all_to_all | solution.py:23
  1074.5 369.4 %all-to-all-start.6 = ((bf16[16,2,4096]{2,1,0:T(2,128)(2,1)}), bf16[16,2,4096]{2,1,0:T(2,128)(2,1)S(1)}, u32[]{:S(2)}, u32[]{:S(2)}) async-start(bf16[16,2,4096]{2,1,0:T(2,128)(2,1)} %reshape.253), calls=%async_computation.6 | async-start | bytes 524288 | tf_op jit(solution)/shard_map/all_to_all | solution.py:60
  1099.2 17.7 %copy-start.9 = (bf16[16,16]{1,0:T(8,128)(2,1)S(1)}, bf16[16,16]{1,0:T(8,128)(2,1)}, u32[]{:S(2)}) copy-start(bf16[16,16]{1,0:T(8,128)(2,1)} %param.27) | copy-start | bytes 1540
  1443.9 39.3 %all-to-all-start.8 = ((bf16[16,2,24576]{2,1,0:T(2,128)(2,1)}), bf16[16,2,24576]{2,1,0:T(2,128)(2,1)S(1)}, u32[]{:S(2)}, u32[]{:S(2)}) async-start(bf16[16,2,24576]{2,1,0:T(2,128)(2,1)} %reshape.287), calls=%async_computation.8 | async-start | bytes 3145728 | tf_op jit(solution)/shard_map/all_to_all | solution.py:142
  1482.2 38.2 %copy-start = (bf16[64,4097]{1,0:T(8,128)(2,1)}, bf16[64,4097]{1,0:T(8,128)(2,1)S(1)}, u32[]{:S(2)}) copy-start(bf16[64,4097]{1,0:T(8,128)(2,1)S(1)} %reshape.269) | copy-start | bytes 1573252
  1483.2 63.7 %all-to-all-start.7 = ((bf16[64,16,256]{2,0,1:T(8,128)(2,1)}), bf16[64,16,256]{2,0,1:T(8,128)(2,1)S(1)}, u32[]{:S(2)}, u32[]{:S(2)}) async-start(bf16[64,16,256]{2,0,1:T(8,128)(2,1)} %bitcast.89), calls=%async_computation.7 | async-start | bytes 1048576 | tf_op jit(solution)/shard_map/all_to_all | solution.py:229
  1508.2 89.3 %reduce-scatter.3.cloned.1.call-start = ((), (), s32[]{:S(2)}) async-start(), calls=%async_computation.12 | async-start | bytes 3932160 | tf_op jit(solution)/shard_map/reduce_scatter | solution.py:80
  1554.7 42.9 %slice-start.1 = ((bf16[3,32,512]{2,1,0:T(8,128)(2,1)}), bf16[2,32,512]{2,1,0:T(8,128)(2,1)S(1)}, s32[]{:S(2)}) async-start(bf16[3,32,512]{2,1,0:T(8,128)(2,1)} %param.16), calls=%async_computation.16 | async-start | bytes 131072 | tf_op jit(solution)/shard_map/slice | solution.py:174
  1558.5 73.2 %reduce-scatter.5.cloned.1.call-start = ((), (), s32[]{:S(2)}) async-start(), calls=%async_computation.13 | async-start | bytes 983040 | tf_op jit(solution)/shard_map/reduce_scatter | solution.py:80
  (4 other events, 43.3 us)
Sparse Core Ops, SparseCore 0:
  169.6 81.2 all-gather.8
  253.9 111.8 all-gather.6
  1558.7 38.8 reduce-scatter.2
  1599.9 31.7 reduce-scatter.4
